TPU v7x, 32 devices: a whole 2x2x4 slice. The times are simulated.
32 devices in a mesh: rep: 4 (over z), ep: 8 (over y, x, core).
Axes of the slice: x: 2, y: 2, z: 4, core: 2. Of those that a mesh axis runs over, the one named last changes fastest.
Arguments:
- tokens: bfloat16 [32, 256, 2048], P('rep', 'ep'), may hold values from -6 to 6
- cotangent: bfloat16 [32, 256, 2048], P('rep', 'ep'), may hold values from -6 to 6
- gate_weights: bfloat16 [32, 256, 8], P('rep', 'ep'), may hold values from 0.049804688 to 0.25
- expert_ids: int32 [32, 256, 8], P('rep', 'ep'), may hold values from 0 to 15, all different within a row; in each aligned block of 256 rows (0 to 255, 256 to 511, ..., all dimensions but the last counted through in order) at most 144 rows name the same one
- seq_lengths: int32 [32], P(('rep', 'ep')), may hold values from 1 to 256, 5120 in all
- query_weight: bfloat16 [2048, 2048], P('ep'), may hold values from -0.125 to 0.125
- key_weight: bfloat16 [2048, 2048], P('ep'), may hold values from -0.125 to 0.125
- value_weight: bfloat16 [2048, 2048], P('ep'), may hold values from -0.125 to 0.125
- output_weight: bfloat16 [2048, 2048], P('ep'), may hold values from -0.75 to 0.75
- attn_gain: bfloat16 [2048], P('ep'), may hold values from 0.25 to 1.75
- ffn_gain: bfloat16 [2048], P('ep'), may hold values from 0.25 to 1.75
- query_gain: bfloat16 [128], P('ep'), may hold values from 0.25 to 1.75
- key_gain: bfloat16 [128], P('ep'), may hold values from 0.25 to 1.75
- expert_in: bfloat16 [16, 2048, 2048], P('ep'), may hold values from -0.125 to 0.125
- expert_out: bfloat16 [16, 1024, 2048], P('ep'), may hold values from -0.5 to 0.5
Outputs:
- result: bfloat16 [32, 256, 2048], P('rep', 'ep')
- token_grad: bfloat16 [32, 256, 2048], P('rep', 'ep')
- query_weight_grad: float32 [2048, 2048], P('ep')
- key_weight_grad: float32 [2048, 2048], P('ep')
- value_weight_grad: float32 [2048, 2048], P('ep')
- output_weight_grad: float32 [2048, 2048], P('ep')
- attn_gain_grad: float32 [2048], P('ep')
- ffn_gain_grad: float32 [2048], P('ep')
- query_gain_grad: float32 [128], P('ep')
- key_gain_grad: float32 [128], P('ep')
- expert_in_grad: float32 [16, 2048, 2048], P('ep', 'rep')
- expert_out_grad: float32 [16, 1024, 2048], P('ep', 'rep')
Inputs may be any that keep to these rules, and one draw needn't show every extreme that they name: `expert_ids`: each token names 8 different experts; within the 256 token slots of one sequence no expert is named more than 144 times, and some expert of some sequence is named exactly 144 times. `seq_lengths`: some sequence is full, with exactly 256 live tokens; live tokens come first in a sequence.
All inputs are finite; a program needn't handle non-finite values. No bound on the sum of `seq_lengths` on one device may be relied on, other than what follows from the above.
Results may differ from a plain program's by a relative error of at most 0.028.
Values may be sent and summed in bfloat16 or wider, within the bound.
A program may use at most 320 MiB of HBM per device.

v0:
```python
import jax
import jax.numpy as jnp
from jax import lax
from jax.sharding import PartitionSpec as P

HEADS = 16
HEAD_DIM = 128
epsilon = 1e-06
rope_base = 50000.0


def rms_norm(values, gain_vector):
    return (
        values
        * lax.rsqrt(jnp.mean(values * values, axis=-1, keepdims=True) + epsilon)
        * gain_vector
    )


def rotary_tables(length, head_width):
    half_width = head_width // 2
    frequency = rope_base ** (-(jnp.arange(half_width, dtype=jnp.float32) * (2.0 / head_width)))
    angles = jnp.arange(length, dtype=jnp.float32)[:, None] * frequency[None, :]
    angles = jnp.concatenate([angles, angles], axis=-1)
    return (jnp.cos(angles)[:, None, :], jnp.sin(angles)[:, None, :])


def rotate(values, cos_table, sin_table):
    half_width = values.shape[-1] // 2
    turned = jnp.concatenate([-values[..., half_width:], values[..., :half_width]], axis=-1)
    return values * cos_table + turned * sin_table


def slot_index(expert_ids, experts, capacity):
    flat_ids = expert_ids.reshape(-1)
    choose = (flat_ids[:, None] == jnp.arange(experts, dtype=jnp.int32)[None, :]).astype(jnp.int32)
    before = jnp.cumsum(choose, axis=0) - choose
    ranking = jnp.sum(before * choose, axis=1)
    return flat_ids * capacity + ranking


def contract(left_side, right_side, left_dim, right_dim):
    return lax.dot_general(
        left_side,
        right_side,
        (((left_dim,), (right_dim,)), ((), ())),
        preferred_element_type=jnp.float32,
    )


def masked_scores(query_low, key_low, living, score_scale):
    raw_scores = (
        jnp.einsum("qhd,khd->hqk", query_low, key_low, preferred_element_type=jnp.float32)
        * score_scale
    )
    return jnp.where(living[None, None, :] > 0.5, raw_scores, -1000000000.0)


def shards(
    tokens,
    cotangent,
    gate_weights,
    expert_ids,
    seq_lengths,
    query_weight,
    key_weight,
    value_weight,
    output_weight,
    attn_gain,
    ffn_gain,
    query_gain,
    key_gain,
    expert_in,
    expert_out,
):
    ep_count = lax.axis_size("ep")
    dealt_arrays = (
        lax.all_to_all(tokens, "ep", split_axis=0, concat_axis=1, tiled=True),
        lax.all_to_all(cotangent, "ep", split_axis=0, concat_axis=1, tiled=True),
        lax.all_to_all(gate_weights, "ep", split_axis=0, concat_axis=1, tiled=True),
    )
    seq_tokens = dealt_arrays[0][0]
    seq_cot = dealt_arrays[1][0]
    seq_gates = dealt_arrays[2][0]
    seq_ids = lax.all_to_all(expert_ids, "ep", split_axis=0, concat_axis=1, tiled=True)[0]
    length = seq_tokens.shape[0]
    model_width = seq_tokens.shape[1]
    top_count = seq_gates.shape[1]
    local_experts = expert_in.shape[0]
    hidden_size = expert_out.shape[1]
    experts = local_experts * ep_count
    capacity = length * top_count * 9 // (8 * experts)
    score_scale = HEAD_DIM ** (-0.5)
    gathered_weights = (
        lax.all_gather(query_weight, "ep", axis=0, tiled=True),
        lax.all_gather(key_weight, "ep", axis=0, tiled=True),
        lax.all_gather(value_weight, "ep", axis=0, tiled=True),
        lax.all_gather(output_weight, "ep", axis=0, tiled=True),
        lax.all_gather(attn_gain, "ep", axis=0, tiled=True),
        lax.all_gather(ffn_gain, "ep", axis=0, tiled=True),
        lax.all_gather(query_gain, "ep", axis=0, tiled=True),
        lax.all_gather(key_gain, "ep", axis=0, tiled=True),
    )
    w_query = gathered_weights[0]
    w_key = gathered_weights[1]
    w_value = gathered_weights[2]
    w_output = gathered_weights[3]
    gain_attn = gathered_weights[4].astype(jnp.float32)
    gain_ffn = gathered_weights[5].astype(jnp.float32)
    gain_query = gathered_weights[6].astype(jnp.float32)
    gain_key = gathered_weights[7].astype(jnp.float32)
    positions = jnp.arange(length, dtype=jnp.int32)
    living = (positions < seq_lengths[0]).astype(jnp.float32)
    combine_weight = seq_gates.astype(jnp.float32) * living[:, None]
    destination = slot_index(seq_ids, experts, capacity)
    pair_count = length * top_count
    token_of_slot = (
        jnp.zeros((experts * capacity,), jnp.int32)
        .at[destination]
        .set(jnp.arange(pair_count, dtype=jnp.int32) // top_count)
    )
    slot_weight = (
        jnp.zeros((experts * capacity,), jnp.float32)
        .at[destination]
        .set(combine_weight.reshape(-1))
    )
    slot_filled = (
        jnp.zeros((experts * capacity,), jnp.bfloat16)
        .at[destination]
        .set(jnp.ones((pair_count,), jnp.bfloat16))
    )
    cos_table, sin_table = rotary_tables(length, HEAD_DIM)

    def head_piece(inputs_pre, gain_vector):
        return rotate(rms_norm(inputs_pre, gain_vector), cos_table, sin_table)

    residual_in = seq_tokens.astype(jnp.float32)
    normed = rms_norm(residual_in, gain_attn).astype(jnp.bfloat16)
    query_pre = jnp.dot(normed, w_query, preferred_element_type=jnp.float32).reshape(
        length, HEADS, HEAD_DIM
    )
    key_pre = jnp.dot(normed, w_key, preferred_element_type=jnp.float32).reshape(
        length, HEADS, HEAD_DIM
    )
    value_low = (
        jnp.dot(normed, w_value, preferred_element_type=jnp.float32)
        .astype(jnp.bfloat16)
        .reshape(length, HEADS, HEAD_DIM)
    )
    query_rot, query_pull = jax.vjp(head_piece, query_pre, gain_query)
    key_rot, key_pull = jax.vjp(head_piece, key_pre, gain_key)
    query_low = query_rot.astype(jnp.bfloat16)
    key_low = key_rot.astype(jnp.bfloat16)
    scores = masked_scores(query_low, key_low, living, score_scale)
    log_total = jax.nn.logsumexp(scores, axis=-1, keepdims=True)
    attention_low = jnp.exp(scores - log_total).astype(jnp.bfloat16)
    context = jnp.einsum(
        "hqk,khd->qhd", attention_low, value_low, preferred_element_type=jnp.float32
    )
    context = context.astype(jnp.bfloat16).reshape(length, HEADS * HEAD_DIM)
    attended = jnp.dot(context, w_output, preferred_element_type=jnp.float32) * living[:, None]
    middle = residual_in + attended
    mixed_in = rms_norm(middle, gain_ffn).astype(jnp.bfloat16)
    outgoing = (mixed_in[token_of_slot] * slot_filled[:, None]).reshape(
        ep_count, local_experts, capacity, model_width
    )
    arrived = lax.all_to_all(outgoing, "ep", split_axis=0, concat_axis=2, tiled=True)[0]
    gate_up = jnp.einsum("erd,edf->erf", arrived, expert_in, preferred_element_type=jnp.float32)

    def swiglu(paired):
        return jax.nn.silu(paired[..., :hidden_size]) * paired[..., hidden_size:]

    activated, swiglu_pull = jax.vjp(swiglu, gate_up)
    activated_low = activated.astype(jnp.bfloat16)
    produced = jnp.einsum(
        "erf,efd->erd", activated_low, expert_out, preferred_element_type=jnp.float32
    ).astype(jnp.bfloat16)
    returned = lax.all_to_all(
        produced[None], "ep", split_axis=2, concat_axis=0, tiled=True
    ).reshape(experts * capacity, model_width)
    gathered = returned[destination].reshape(length, top_count, model_width).astype(jnp.float32)
    outcome = middle + jnp.sum(combine_weight[:, :, None] * gathered, axis=1)
    upstream = seq_cot.astype(jnp.float32)
    outgoing_grad = (upstream[token_of_slot] * slot_weight[:, None]).astype(jnp.bfloat16)
    outgoing_grad = outgoing_grad.reshape(ep_count, local_experts, capacity, model_width)
    arrived_grad = lax.all_to_all(outgoing_grad, "ep", split_axis=0, concat_axis=2, tiled=True)[0]
    activated_grad = jnp.einsum(
        "erd,efd->erf", arrived_grad, expert_out, preferred_element_type=jnp.float32
    )
    gate_up_grad = swiglu_pull(activated_grad)[0].astype(jnp.bfloat16)
    out_local_grad = jnp.einsum(
        "erf,erd->efd", activated_low, arrived_grad, preferred_element_type=jnp.float32
    )
    in_local_grad = jnp.einsum(
        "erd,erf->edf", arrived, gate_up_grad, preferred_element_type=jnp.float32
    )
    arrived_back = jnp.einsum(
        "erf,edf->erd", gate_up_grad, expert_in, preferred_element_type=jnp.float32
    ).astype(jnp.bfloat16)
    expert_sums = (
        lax.psum_scatter(
            in_local_grad.astype(jnp.bfloat16), "rep", scatter_dimension=1, tiled=True
        ).astype(jnp.float32),
        lax.psum_scatter(
            out_local_grad.astype(jnp.bfloat16), "rep", scatter_dimension=1, tiled=True
        ).astype(jnp.float32),
    )
    returned_grad = lax.all_to_all(
        arrived_back[None], "ep", split_axis=2, concat_axis=0, tiled=True
    ).reshape(experts * capacity, model_width)
    mixed_grad = jnp.sum(
        returned_grad[destination].reshape(length, top_count, model_width).astype(jnp.float32),
        axis=1,
    )
    ffn_values, ffn_pull = jax.vjp(rms_norm, middle, gain_ffn)
    middle_part, ffn_gain_grad = ffn_pull(mixed_grad)
    middle_grad = upstream + middle_part
    attended_grad = (middle_grad * living[:, None]).astype(jnp.bfloat16)
    output_weight_grad = contract(context, attended_grad, 0, 0)
    context_grad = (
        contract(attended_grad, w_output, 1, 1)
        .astype(jnp.bfloat16)
        .reshape(length, HEADS, HEAD_DIM)
    )
    attention_again = jnp.exp(masked_scores(query_low, key_low, living, score_scale) - log_total)
    attention_again_low = attention_again.astype(jnp.bfloat16)
    value_grad = jnp.einsum(
        "hqk,qhd->khd", attention_again_low, context_grad, preferred_element_type=jnp.float32
    )
    value_grad = value_grad.astype(jnp.bfloat16).reshape(length, HEADS * HEAD_DIM)
    prob_grad = jnp.einsum(
        "qhd,khd->hqk", context_grad, value_low, preferred_element_type=jnp.float32
    )
    score_grad = attention_again * (
        prob_grad - jnp.sum(attention_again * prob_grad, axis=-1, keepdims=True)
    )
    score_grad = score_grad.astype(jnp.bfloat16)
    query_rot_grad = (
        jnp.einsum("hqk,khd->qhd", score_grad, key_low, preferred_element_type=jnp.float32)
        * score_scale
    )
    key_rot_grad = (
        jnp.einsum("hqk,qhd->khd", score_grad, query_low, preferred_element_type=jnp.float32)
        * score_scale
    )
    query_grad, query_gain_grad = query_pull(query_rot_grad)
    key_grad, key_gain_grad = key_pull(key_rot_grad)
    query_grad = query_grad.astype(jnp.bfloat16).reshape(length, HEADS * HEAD_DIM)
    key_grad = key_grad.astype(jnp.bfloat16).reshape(length, HEADS * HEAD_DIM)
    normed_grad = (
        contract(query_grad, w_query, 1, 1)
        + contract(key_grad, w_key, 1, 1)
        + contract(value_grad, w_value, 1, 1)
    )
    query_weight_grad = contract(normed, query_grad, 0, 0)
    key_weight_grad = contract(normed, key_grad, 0, 0)
    value_weight_grad = contract(normed, value_grad, 0, 0)
    attn_values, attn_pull = jax.vjp(rms_norm, residual_in, gain_attn)
    input_part, attn_gain_grad = attn_pull(normed_grad)
    input_grad = (middle_grad + input_part).astype(jnp.bfloat16)
    moved_back = (
        lax.all_to_all(
            outcome.astype(jnp.bfloat16)[None], "ep", split_axis=1, concat_axis=0, tiled=True
        ),
        lax.all_to_all(input_grad[None], "ep", split_axis=1, concat_axis=0, tiled=True),
    )
    shares = (
        lax.psum_scatter(
            query_weight_grad.astype(jnp.bfloat16), "ep", scatter_dimension=0, tiled=True
        ).astype(jnp.float32),
        lax.psum_scatter(
            key_weight_grad.astype(jnp.bfloat16), "ep", scatter_dimension=0, tiled=True
        ).astype(jnp.float32),
        lax.psum_scatter(
            value_weight_grad.astype(jnp.bfloat16), "ep", scatter_dimension=0, tiled=True
        ).astype(jnp.float32),
        lax.psum_scatter(
            output_weight_grad.astype(jnp.bfloat16), "ep", scatter_dimension=0, tiled=True
        ).astype(jnp.float32),
        lax.psum_scatter(
            attn_gain_grad.astype(jnp.bfloat16), "ep", scatter_dimension=0, tiled=True
        ).astype(jnp.float32),
        lax.psum_scatter(
            ffn_gain_grad.astype(jnp.bfloat16), "ep", scatter_dimension=0, tiled=True
        ).astype(jnp.float32),
        lax.psum_scatter(
            query_gain_grad.astype(jnp.bfloat16), "ep", scatter_dimension=0, tiled=True
        ).astype(jnp.float32),
        lax.psum_scatter(
            key_gain_grad.astype(jnp.bfloat16), "ep", scatter_dimension=0, tiled=True
        ).astype(jnp.float32),
    )
    shares = (
        lax.psum(shares[0].astype(jnp.bfloat16), "rep").astype(jnp.float32),
        lax.psum(shares[1].astype(jnp.bfloat16), "rep").astype(jnp.float32),
        lax.psum(shares[2].astype(jnp.bfloat16), "rep").astype(jnp.float32),
        lax.psum(shares[3].astype(jnp.bfloat16), "rep").astype(jnp.float32),
        lax.psum(shares[4].astype(jnp.bfloat16), "rep").astype(jnp.float32),
        lax.psum(shares[5].astype(jnp.bfloat16), "rep").astype(jnp.float32),
        lax.psum(shares[6].astype(jnp.bfloat16), "rep").astype(jnp.float32),
        lax.psum(shares[7].astype(jnp.bfloat16), "rep").astype(jnp.float32),
    )
    return (
        moved_back[0],
        moved_back[1],
        shares[0],
        shares[1],
        shares[2],
        shares[3],
        shares[4],
        shares[5],
        shares[6],
        shares[7],
        expert_sums[0],
        expert_sums[1],
    )


def solution(mesh):
    return jax.shard_map(
        shards,
        mesh=mesh,
        in_specs=(
            P("rep", "ep", None),
            P("rep", "ep", None),
            P("rep", "ep", None),
            P("rep", "ep", None),
            P(("rep", "ep")),
            P("ep", None),
            P("ep", None),
            P("ep", None),
            P("ep", None),
            P("ep"),
            P("ep"),
            P("ep"),
            P("ep"),
            P("ep", None, None),
            P("ep", None, None),
        ),
        out_specs=(
            P("rep", "ep", None),
            P("rep", "ep", None),
            P("ep", None),
            P("ep", None),
            P("ep", None),
            P("ep", None),
            P("ep"),
            P("ep"),
            P("ep"),
            P("ep"),
            P("ep", "rep", None),
            P("ep", "rep", None),
        ),
        check_vma=False,
    )
```

profile of v0, /device:TPU:0, one launch (start us, length us, event | category | flops | bytes accessed | tf_op | source)
XLA Modules:
  0.0 1802.4 jit_solution(4447141272363571093)
XLA Ops:
  24.0 9.7 all-gather
  35.4 13.8 all-reduce.13
  49.2 9.2 all-gather.1
  69.8 8.1 all-to-all-done
  82.2 8.1 scatter_custom_fusion
  90.3 14.6 scatter_custom_fusion.1
  105.0 8.1 scatter_custom_fusion.2
  115.5 11.5 gather_fusion.2
  127.0 10.1 multiply_convert_fusion
  142.9 11.9 copy.101
  154.8 12.5 copy.102
  183.2 71.8 %all-gather.7.cloned.1.call-done = bf16[2048,2048]{1,0:T(8,128)(2,1)} async-done(((bf16[256,2048]{1,0:T(8,128)(2,1)}), bf16[2048,2048]{1,0:T(8,128)(2,1)}) %all-gather.7.cloned.1.call-update) | async-done | bytes 8388624 | tf_op jit(solution)/shard_map/all_gather | solution.py:97
  263.1 66.4 %all-gather.13.cloned.1.call-done = bf16[2048,2048]{1,0:T(8,128)(2,1)} async-done(((bf16[256,2048]{1,0:T(8,128)(2,1)}), bf16[2048,2048]{1,0:T(8,128)(2,1)}) %all-gather.13.cloned.1.call-update) | async-done | bytes 8388624 | tf_op jit(solution)/shard_map/all_gather | solution.py:98
  329.5 15.4 multiply_reduce_fusion.7
  346.5 9.8 gather_fusion
  356.3 8.0 broadcast_multiply_fusion
  369.5 9.2 copy.118
  378.7 96.1 %all-to-all-done.3 = bf16[8,2,144,2048]{3,2,1,0:T(8,128)(2,1)} async-done(((bf16[8,2,144,2048]{3,2,1,0:T(8,128)(2,1)}), bf16[8,2,144,2048]{3,2,1,0:T(8,128)(2,1)}, u32[]{:S(2)}, u32[]{:S(2)}) %all-to-all-start.3) | async-done | bytes 9437216 | tf_op jit(solution)/shard_map/all_to_all | solution.py:167
  474.8 9.2 copy.112
  484.0 27.4 %fusion.66 = f32[2,1152,2048]{2,1,0:T(8,128)} fusion(bf16[2,1152,2048]{2,1,0:T(8,128)(2,1)} %bitcast.188, bf16[2,2048,2048]{2,1,0:T(8,128)(2,1)} %param.28), kind=kOutput, calls=%fused_computation.165 | convolution fusion | flops 19327352832 | bytes 45088768 | tf_op jit(solution)/shard_map/erd,edf->erf/dot_general | solution.py:168
  511.4 27.5 %fusion.31 = (f32[2,1152,1024]{2,1,0:T(8,128)}, f32[2,1152,1024]{2,1,0:T(8,128)}, bf16[2,1152,1024]{2,1,0:T(8,128)(2,1)}) fusion(f32[2,1152,2048]{2,1,0:T(8,128)} %fusion.66, bf16[2,1152,2048]{2,1,0:T(8,128)(2,1)} %bitcast.190, bf16[2,1024,2048]{2,1,0:T(8,128)(2,1)} %param.29), kind=kOutput, calls=%fused_computation.95 | convolution fusion | flops 9696706560 | bytes 60293120 | tf_op jit(solution)/shard_map/erd,efd->erf/dot_general | solution.py:187
  538.8 14.6 fusion.4
  553.5 27.9 %copy.113 = bf16[1,2,1152,2048]{3,1,0,2:T(2,128)(2,1)} copy(bf16[1,2,1152,2048]{3,2,1,0:T(8,128)(2,1)S(1)} %fusion.4) | data formatting | bytes 18874368 | tf_op jit(solution)/shard_map/broadcast_in_dim | solution.py:179
  586.5 27.6 %fusion.5 = bf16[1,2,1152,2048]{3,2,1,0:T(8,128)(2,1)} fusion(bf16[2,2048,2048]{2,1,0:T(8,128)(2,1)} %param.28, f32[2,1152,1024]{2,1,0:T(8,128)} %get-tuple-element.37, f32[2,1152,1024]{2,1,0:T(8,128)} %get-tuple-element.36), kind=kOutput, calls=%fused_computation.22 | convolution fusion | flops 19341508608 | bytes 45088768 | tf_op jit(solution)/shard_map/erf,edf->erd/dot_general | solution.py:197
  614.1 18.2 %copy.119 = bf16[1,2,1152,2048]{3,1,0,2:T(2,128)(2,1)} copy(bf16[1,2,1152,2048]{3,2,1,0:T(8,128)(2,1)} %fusion.5) | data formatting | bytes 18874368 | tf_op jit(solution)/shard_map/broadcast_in_dim | solution.py:209
  632.3 59.5 %all-to-all-done.4 = bf16[1,2,1152,2048]{3,1,0,2:T(2,128)(2,1)} async-done(((bf16[1,2,1152,2048]{3,1,0,2:T(2,128)(2,1)}), bf16[1,2,1152,2048]{3,1,0,2:T(2,128)(2,1)}, u32[]{:S(2)}, u32[]{:S(2)}) %all-to-all-start.4) | async-done | bytes 9437216 | tf_op jit(solution)/shard_map/all_to_all | solution.py:178
  697.3 11.7 copy.114
  709.0 93.1 %all-to-all-done.8 = bf16[1,2,1152,2048]{3,1,0,2:T(2,128)(2,1)} async-done(((bf16[1,2,1152,2048]{3,1,0,2:T(2,128)(2,1)}), bf16[1,2,1152,2048]{3,1,0,2:T(2,128)(2,1)}, u32[]{:S(2)}, u32[]{:S(2)}) %all-to-all-start.8) | async-done | bytes 9437216 | tf_op jit(solution)/shard_map/all_to_all | solution.py:208
  802.1 11.8 copy.120
  813.9 21.2 %gather_fusion.1 = bf16[2048,2048]{1,0:T(8,128)(2,1)} fusion(bf16[2304,2048]{1,0:T(8,128)(2,1)} %bitcast.178, s32[2048]{0:T(1024)S(1)} %broadcast_clamp_fusion), kind=kCustom, calls=%fused_computation.1 | custom fusion | bytes 16785408 | tf_op jit(solution)/shard_map/gather | solution.py:181
  835.1 21.4 %gather_fusion.3 = bf16[2048,2048]{1,0:T(8,128)(2,1)} fusion(bf16[2304,2048]{1,0:T(8,128)(2,1)} %bitcast.179, s32[2048]{0:T(1024)S(1)} %broadcast_clamp_fusion), kind=kCustom, calls=%fused_computation.3 | custom fusion | bytes 16785408 | tf_op jit(solution)/shard_map/gather | solution.py:212
  856.5 11.4 convert_reduce_fusion
  870.1 12.9 fusion
  906.9 7.7 convolution_convert_fusion.3
  947.4 17.9 convolution_convert_fusion.7
  965.3 10.8 reduce-scatter.11.cloned.1.call-done
  976.2 74.9 %reduce-scatter.13.cloned.1.call-done = bf16[256,2048]{1,0:T(8,128)(2,1)} async-done(((bf16[2048,2048]{1,0:T(8,128)(2,1)}), bf16[256,2048]{1,0:T(8,128)(2,1)}) %reduce-scatter.13.cloned.1.call-update) | async-done | bytes 1048592 | tf_op jit(solution)/shard_map/reduce_scatter | solution.py:277
  1051.0 75.0 %reduce-scatter.9.cloned.1.call-done = bf16[256,2048]{1,0:T(8,128)(2,1)} async-done(((bf16[2048,2048]{1,0:T(8,128)(2,1)}), bf16[256,2048]{1,0:T(8,128)(2,1)}) %reduce-scatter.9.cloned.1.call-update) | async-done | bytes 1048592 | tf_op jit(solution)/shard_map/reduce_scatter | solution.py:271
  1126.0 75.6 %reduce-scatter.7.cloned.1.call-done = bf16[256,2048]{1,0:T(8,128)(2,1)} async-done(((bf16[2048,2048]{1,0:T(8,128)(2,1)}), bf16[256,2048]{1,0:T(8,128)(2,1)}) %reduce-scatter.7.cloned.1.call-update) | async-done | bytes 1048592 | tf_op jit(solution)/shard_map/reduce_scatter | solution.py:268
  1201.7 29.4 %convolution_convert_fusion = bf16[2,2048,2048]{2,1,0:T(8,128)(2,1)} fusion(bf16[2,1152,2048]{2,1,0:T(8,128)(2,1)} %bitcast.189, f32[2,1152,1024]{2,1,0:T(8,128)} %get-tuple-element.37, f32[2,1152,1024]{2,1,0:T(8,128)} %get-tuple-element.36), kind=kOutput, calls=%fused_computation.13 | convolution fusion | flops 19345178624 | bytes 45088768 | tf_op jit(solution)/shard_map/erd,erf->edf/dot_general | solution.py:194
  1249.9 8.0 reduce.8
  1266.4 6.8 reduce.7
  1285.0 21.1 %all-reduce.12 = (bf16[2048]{0:T(1024)(128)(2,1)S(1)}, bf16[2048]{0:T(1024)(128)(2,1)S(1)}, bf16[128]{0:T(256)(128)(2,1)S(1)}, bf16[128]{0:T(256)(128)(2,1)S(1)}) all-reduce(bf16[2048]{0:T(1024)(128)(2,1)S(1)} %get-tuple-element.18, bf16[2048]{0:T(1024)(128)(2,1)S(1)} %get-tuple-element.16, ...), channel_id=6, replica_groups=mesh['rep'=4,'ep'=8] {'ep'}, use_global_device_ids=true, to_apply=%region_28.29.clone | all-reduce | flops 4352 | bytes 17408
  1306.5 12.4 all-reduce.14
  1329.6 19.3 %reduce-scatter.17.cloned.1.call-done = bf16[2,256,2048]{2,1,0:T(8,128)(2,1)} async-done(((bf16[2,1024,2048]{2,1,0:T(8,128)(2,1)}), bf16[2,256,2048]{2,1,0:T(8,128)(2,1)}) %reduce-scatter.17.cloned.1.call-update) | async-done | bytes 2097168 | tf_op jit(solution)/shard_map/reduce_scatter | solution.py:204
  1353.0 153.9 %all-reduce.18.cloned.1.call-done = (bf16[256,2048]{1,0:T(8,128)(2,1)}, bf16[256,2048]{1,0:T(8,128)(2,1)}, bf16[256,2048]{1,0:T(8,128)(2,1)}, bf16[256,2048]{1,0:T(8,128)(2,1)}) async-done(((bf16[256,2048]{1,0:T(8,128)(2,1)}, bf16[256,2048]{1,0:T(8,128)(2,1)}, bf16[256,2048]{1,0:T(8,128)(2,1)}, bf16[256,2048]{1,0:T(8,128)(2,1)}), (bf16[256,2048]{1,0:T(8,128)(2,1)}, bf16[256,2048]{1,0:T(8,128)(2,1)}, ...) | async-done | bytes 4194320 | tf_op jit(solution)/shard_map/psum | solution.py:294
  1515.8 273.0 %reduce-scatter.15.cloned.1.call-done = bf16[2,512,2048]{2,1,0:T(8,128)(2,1)} async-done(((bf16[2,2048,2048]{2,1,0:T(8,128)(2,1)}), bf16[2,512,2048]{2,1,0:T(8,128)(2,1)}) %reduce-scatter.15.cloned.1.call-update) | async-done | bytes 4194320 | tf_op jit(solution)/shard_map/reduce_scatter | solution.py:201
  1788.8 6.7 convert_element_type.294
  (322 shorter events, 202.1 us)
Async XLA Ops:
  7.2 26.5 %copy-start.73 = (u32[32]{0:T(128)S(1)}, u32[32]{0:T(128)}, u32[]{:S(2)}) copy-start(u32[32]{0:T(128)} %constant.91) | copy-start | bytes 388
  7.2 16.7 copy-start.74
  7.2 27.7 %copy-start.75 = (bf16[16]{0:T(256)(128)(2,1)S(1)}, bf16[16]{0:T(256)(128)(2,1)}, u32[]{:S(2)}) copy-start(bf16[16]{0:T(256)(128)(2,1)} %param.26) | copy-start | bytes 100
  7.2 28.0 %copy-start.76 = (bf16[16]{0:T(256)(128)(2,1)S(1)}, bf16[16]{0:T(256)(128)(2,1)}, u32[]{:S(2)}) copy-start(bf16[16]{0:T(256)(128)(2,1)} %param.27) | copy-start | bytes 100
  7.2 42.0 %copy-start.77 = (bf16[256]{0:T(256)(128)(2,1)S(1)}, bf16[256]{0:T(256)(128)(2,1)}, u32[]{:S(2)}) copy-start(bf16[256]{0:T(256)(128)(2,1)} %param.25) | copy-start | bytes 1540
  7.3 135.6 %all-gather.9.cloned.1.call-start = ((), (), s32[]{:S(2)}) async-start(), calls=%async_computation.17 | async-start | bytes 9437184 | tf_op jit(solution)/shard_map/all_gather | solution.py:95
  8.0 146.8 %all-gather.11.cloned.1.call-start = ((), (), s32[]{:S(2)}) async-start(), calls=%async_computation.18 | async-start | bytes 9437184 | tf_op jit(solution)/shard_map/all_gather | solution.py:96
  8.7 246.3 %all-gather.7.cloned.1.call-start = ((), (), s32[]{:S(2)}) async-start(), calls=%async_computation.16 | async-start | bytes 9437184 | tf_op jit(solution)/shard_map/all_gather | solution.py:97
  9.5 320.0 %all-gather.13.cloned.1.call-start = ((), (), s32[]{:S(2)}) async-start(), calls=%async_computation.19 | async-start | bytes 9437184 | tf_op jit(solution)/shard_map/all_gather | solution.py:98
  10.7 9.8 all-to-all-start.1
  17.9 311.6 %copy-start.59 = (f32[256]{0:T(256)}, f32[256]{0:T(256)S(1)}, u32[]{:S(2)}) copy-start(f32[256]{0:T(256)S(1)} %compare_convert_fusion) | copy-start | bytes 3076
  20.6 38.4 %all-to-all-start.2 = ((s32[8,1,256]{2,1,0:T(1,128)}), s32[8,1,256]{2,1,0:T(1,128)S(1)}, u32[]{:S(2)}, u32[]{:S(2)}) async-start(s32[8,1,256]{2,1,0:T(1,128)} %reshape.509), calls=%async_computation.2 | async-start | bytes 16384 | tf_op jit(solution)/shard_map/all_to_all | solution.py:85
  23.9 237.0 %copy-start.67 = (pred[256]{0:T(512)(128)(4,1)}, pred[256]{0:T(512)(128)(4,1)S(1)}, u32[]{:S(2)}) copy-start(pred[256]{0:T(512)(128)(4,1)S(1)} %broadcast_compare_fusion) | copy-start | bytes 772
  33.6 108.9 %copy-start.45 = (f32[8,1,256]{2,1,0:T(1,128)}, f32[8,1,256]{2,1,0:T(1,128)S(1)}, u32[]{:S(2)}) copy-start(f32[8,1,256]{2,1,0:T(1,128)S(1)} %convert_element_type.303) | copy-start | bytes 24580
  49.2 127.7 %copy-start.69 = (f32[128]{0:T(128)}, f32[128]{0:T(128)S(1)}, u32[]{:S(2)}) copy-start(f32[128]{0:T(128)S(1)} %convert_element_type.242) | copy-start | bytes 1540
  49.2 127.6 %copy-start.71 = (f32[128]{0:T(128)}, f32[128]{0:T(128)S(1)}, u32[]{:S(2)}) copy-start(f32[128]{0:T(128)S(1)} %convert_element_type.244) | copy-start | bytes 1540
  58.5 286.5 %copy-start.47 = (f32[8,1,256]{2,1,0:T(1,128)}, f32[8,1,256]{2,1,0:T(1,128)S(1)}, u32[]{:S(2)}) copy-start(f32[8,1,256]{2,1,0:T(1,128)S(1)} %convert_element_type.304) | copy-start | bytes 24580
  59.0 18.9 %all-to-all-start = ((bf16[8,32,2048]{2,1,0:T(8,128)(2,1)}), bf16[8,32,2048]{2,1,0:T(8,128)(2,1)S(1)}, u32[]{:S(2)}, u32[]{:S(2)}) async-start(bf16[8,32,2048]{2,1,0:T(8,128)(2,1)} %param.15), calls=%async_computation | async-start | bytes 2097152 | tf_op jit(solution)/shard_map/all_to_all | solution.py:78
  77.9 251.6 %copy-start.3 = (bf16[8,32,2048]{2,1,0:T(8,128)(2,1)}, bf16[8,32,2048]{2,1,0:T(8,128)(2,1)S(1)}, u32[]{:S(2)}) copy-start(bf16[8,32,2048]{2,1,0:T(8,128)(2,1)S(1)} %all-to-all-done) | copy-start | bytes 3145732
  77.9 36.2 %all-to-all-start.6 = ((bf16[8,32,2048]{2,1,0:T(8,128)(2,1)}), bf16[8,32,2048]{2,1,0:T(8,128)(2,1)}, u32[]{:S(2)}, u32[]{:S(2)}) async-start(bf16[8,32,2048]{2,1,0:T(8,128)(2,1)} %param.16), calls=%async_computation.6 | async-start | bytes 2097152 | tf_op jit(solution)/shard_map/all_to_all | solution.py:79
  82.2 22.8 %copy-start.54 = (s32[2048,1]{0,1:T(1,128)}, s32[2048,1]{0,1:T(1,128)S(1)}, u32[]{:S(2)}) copy-start(s32[2048,1]{0,1:T(1,128)S(1)} %compare_select_fusion) | copy-start | bytes 24580
  114.1 28.4 %copy-start.61 = (f32[256]{0:T(256)}, f32[256]{0:T(256)S(1)}, u32[]{:S(2)}) copy-start(f32[256]{0:T(256)S(1)} %rsqrt.45) | copy-start | bytes 3076
  137.1 227.2 %all-to-all-start.7 = ((bf16[8,2,144,2048]{3,2,1,0:T(8,128)(2,1)}), bf16[8,2,144,2048]{3,2,1,0:T(8,128)(2,1)}, u32[]{:S(2)}, u32[]{:S(2)}) async-start(bf16[8,2,144,2048]{3,2,1,0:T(8,128)(2,1)} %multiply_convert_fusion), calls=%async_computation.7 | async-start | bytes 18874368 | tf_op jit(solution)/shard_map/all_to_all | solution.py:186
  142.5 31.3 %copy-start.7 = (bf16[8,32,2048]{2,1,0:T(8,128)(2,1)}, bf16[8,32,2048]{2,1,0:T(8,128)(2,1)S(1)}, u32[]{:S(2)}) copy-start(bf16[8,32,2048]{2,1,0:T(8,128)(2,1)S(1)} %fusion.28) | copy-start | bytes 3145732
  183.2 77.7 %copy-start.41 = (f32[16,256]{1,0:T(8,128)}, f32[16,256]{1,0:T(8,128)S(1)}, u32[]{:S(2)}) copy-start(f32[16,256]{1,0:T(8,128)S(1)} %log_add_fusion) | copy-start | bytes 49156
  263.1 81.9 %copy-start.21 = (bf16[16,128,256]{2,1,0:T(8,128)(2,1)}, bf16[16,128,256]{2,1,0:T(8,128)(2,1)S(1)}, u32[]{:S(2)}) copy-start(bf16[16,128,256]{2,1,0:T(8,128)(2,1)S(1)} %convolution_convert_fusion.11) | copy-start | bytes 3145732
  344.9 11.4 copy-start.63
  345.0 11.4 copy-start.56
  364.3 110.4 %all-to-all-start.3 = ((bf16[8,2,144,2048]{3,2,1,0:T(8,128)(2,1)}), bf16[8,2,144,2048]{3,2,1,0:T(8,128)(2,1)}, u32[]{:S(2)}, u32[]{:S(2)}) async-start(bf16[8,2,144,2048]{3,2,1,0:T(8,128)(2,1)} %broadcast_multiply_fusion), calls=%async_computation.3 | async-start | bytes 18874368 | tf_op jit(solution)/shard_map/all_to_all | solution.py:167
  581.4 110.4 %all-to-all-start.4 = ((bf16[1,2,1152,2048]{3,1,0,2:T(2,128)(2,1)}), bf16[1,2,1152,2048]{3,1,0,2:T(2,128)(2,1)}, u32[]{:S(2)}, u32[]{:S(2)}) async-start(bf16[1,2,1152,2048]{3,1,0,2:T(2,128)(2,1)} %copy.113), calls=%async_computation.4 | async-start | bytes 18874368 | tf_op jit(solution)/shard_map/all_to_all | solution.py:178
  632.3 64.7 %copy-start.44 = (bf16[8,8,32]{2,1,0:T(8,128)(2,1)S(1)}, bf16[8,8,32]{2,1,0:T(8,128)(2,1)}, u32[]{:S(2)}) copy-start(bf16[8,8,32]{2,1,0:T(8,128)(2,1)} %copy-done.43) | copy-start | bytes 12292
  632.3 64.8 %copy-start.60 = (f32[256]{0:T(256)S(1)}, f32[256]{0:T(256)}, u32[]{:S(2)}) copy-start(f32[256]{0:T(256)} %copy-done.59) | copy-start | bytes 3076
  632.3 65.0 %copy-start.55 = (s32[2048,1]{0,1:T(1,128)S(1)}, s32[2048,1]{0,1:T(1,128)}, u32[]{:S(2)}) copy-start(s32[2048,1]{0,1:T(1,128)} %copy-done.54) | copy-start | bytes 24580
  691.8 110.3 %all-to-all-start.8 = ((bf16[1,2,1152,2048]{3,1,0,2:T(2,128)(2,1)}), bf16[1,2,1152,2048]{3,1,0,2:T(2,128)(2,1)}, u32[]{:S(2)}, u32[]{:S(2)}) async-start(bf16[1,2,1152,2048]{3,1,0,2:T(2,128)(2,1)} %copy.119), calls=%async_computation.8 | async-start | bytes 18874368 | tf_op jit(solution)/shard_map/all_to_all | solution.py:208
  696.8 279.3 %reduce-scatter.11.cloned.1.call-start = ((), (), s32[]{:S(2)}) async-start(), calls=%async_computation.22 | async-start | bytes 9437184 | tf_op jit(solution)/shard_map/reduce_scatter | solution.py:274
  856.5 11.5 copy-start.6
  856.5 11.4 copy-start.48
  856.5 11.4 copy-start.57
  905.3 145.7 %reduce-scatter.13.cloned.1.call-start = ((), (), s32[]{:S(2)}) async-start(), calls=%async_computation.23 | async-start | bytes 9437184 | tf_op jit(solution)/shard_map/reduce_scatter | solution.py:277
  914.6 211.4 %reduce-scatter.9.cloned.1.call-start = ((), (), s32[]{:S(2)}) async-start(), calls=%async_computation.21 | async-start | bytes 9437184 | tf_op jit(solution)/shard_map/reduce_scatter | solution.py:271
  937.6 264.0 %reduce-scatter.7.cloned.1.call-start = ((), (), s32[]{:S(2)}) async-start(), calls=%async_computation.20 | async-start | bytes 9437184 | tf_op jit(solution)/shard_map/reduce_scatter | solution.py:268
  947.3 401.6 %reduce-scatter.17.cloned.1.call-start = ((), (), s32[]{:S(2)}) async-start(), calls=%async_computation.25 | async-start | bytes 10485760 | tf_op jit(solution)/shard_map/reduce_scatter | solution.py:204
  965.3 541.7 %all-reduce.18.cloned.1.call-start = ((), (), s32[]{:S(2)}) async-start(), calls=%async_computation.26 | async-start | bytes 8388608 | tf_op jit(solution)/shard_map/psum | solution.py:294
  1201.6 587.2 %reduce-scatter.15.cloned.1.call-start = ((), (), s32[]{:S(2)}) async-start(), calls=%async_computation.24 | async-start | bytes 20971520 | tf_op jit(solution)/shard_map/reduce_scatter | solution.py:201
  1232.3 12.0 slice-start
  1249.4 15.4 copy-start.22
  1260.5 19.6 %all-to-all-start.9 = ((bf16[8,2,32768]{2,1,0:T(2,128)(2,1)}), bf16[8,2,32768]{2,1,0:T(2,128)(2,1)}, u32[]{:S(2)}, u32[]{:S(2)}) async-start(bf16[8,2,32768]{2,1,0:T(2,128)(2,1)} %reshape.515), calls=%async_computation.9 | async-start | bytes 2097152 | tf_op jit(solution)/shard_map/all_to_all | solution.py:265
  1280.2 46.8 %all-to-all-start.5 = ((bf16[8,2,32768]{2,1,0:T(2,128)(2,1)}), bf16[8,2,32768]{2,1,0:T(2,128)(2,1)S(1)}, u32[]{:S(2)}, u32[]{:S(2)}) async-start(bf16[8,2,32768]{2,1,0:T(2,128)(2,1)} %reshape.513), calls=%async_computation.5 | async-start | bytes 2097152 | tf_op jit(solution)/shard_map/all_to_all | solution.py:262
  (53 other events, 179.0 us)
Sparse Core Ops, SparseCore 0:
  9.9 57.3 all-gather.8
  69.2 65.4 all-gather.10
  136.5 118.4 all-gather.6
  256.7 72.6 all-gather.12
  905.4 70.6 reduce-scatter.10
  979.5 71.5 reduce-scatter.12
  1054.5 71.5 reduce-scatter.8
  1130.1 71.4 reduce-scatter.6
  1204.0 144.8 reduce-scatter.16
  1351.3 155.5 all-reduce.17
  1509.3 279.4 reduce-scatter.14
where the time goes:
time: 1810 us; the launch traced here: 1800 us
  waiting for transfers between devices  1090 us (60%)
  local copies, waits for them, and re-layouts  247 us (14%)
  matrix products  231 us (13%)
  other arithmetic  106 us (6%)
  blocking collectives  66.2 us (4%)
  starting transfers between devices  45.7 us (3%)
  between operations  18.4 us (1%)
    reduce_scatter x1, waiting for transfers between devices, shards(): lax.psum_scatter(in_local_grad.astype(jnp.bfloat16), 'rep', scatter_dimen...  273 us
    psum x1, waiting for transfers between devices, shards(): lax.psum(shares[0].astype(jnp.bfloat16), 'rep').astype(jnp.float32)  154 us
    all_to_all x1, waiting for transfers between devices, shards(): lax.all_to_all(outgoing, 'ep', split_axis=0, concat_axis=2, tiled=True)[0]  96.1 us
    all_to_all x1, waiting for transfers between devices, shards(): lax.all_to_all(arrived_back[None], 'ep', split_axis=2, concat_axis=0, til...  93.1 us
    reduce_scatter x1, waiting for transfers between devices, shards(): lax.psum_scatter(query_weight_grad.astype(jnp.bfloat16), 'ep', scatter_di...  75.6 us
    reduce_scatter x1, waiting for transfers between devices, shards(): lax.psum_scatter(key_weight_grad.astype(jnp.bfloat16), 'ep', scatter_dime...  75 us
    reduce_scatter x1, waiting for transfers between devices, shards(): lax.psum_scatter(output_weight_grad.astype(jnp.bfloat16), 'ep', scatter_d...  74.9 us
    all_gather x1, waiting for transfers between devices, shards(): lax.all_gather(value_weight, 'ep', axis=0, tiled=True)  71.8 us
  transfers between devices with their start and end apart: 21, of which 15 were waited for; matrix products, arithmetic and copies ran while one was open for 20% of the time, Pallas kernels for 0%

commit v1 on v0

--- a/solution.py
+++ b/solution.py
@@ -164,7 +164,10 @@
     outgoing = (mixed_in[token_of_slot] * slot_filled[:, None]).reshape(
         ep_count, local_experts, capacity, model_width
     )
-    arrived = lax.all_to_all(outgoing, "ep", split_axis=0, concat_axis=2, tiled=True)[0]
+    arrived = jnp.concatenate(
+        lax.all_to_all(jnp.stack(jnp.split(outgoing, lax.axis_size("ep"), axis=0)), "ep", 0, 0),
+        axis=2,
+    )[0]
     gate_up = jnp.einsum("erd,edf->erf", arrived, expert_in, preferred_element_type=jnp.float32)
 
     def swiglu(paired):

time: 1810 us -> 1830 us (1.011)
    unnamed x182 -> x189, local copies, waits for them, and re-layouts: 34 us -> 41.7 us
where the time goes in v1:
time: 1830 us; the launch traced here: 1820 us
  waiting for transfers between devices  1090 us (60%)
  local copies, waits for them, and re-layouts  261 us (14%)
  matrix products  232 us (13%)
  other arithmetic  106 us (6%)
  blocking collectives  66.2 us (4%)
  starting transfers between devices  45.6 us (2%)
  between operations  18.4 us (1%)
    reduce_scatter x1, waiting for transfers between devices, shards(): lax.psum_scatter(in_local_grad.astype(jnp.bfloat16), 'rep', scatter_dimen...  273 us
    psum x1, waiting for transfers between devices, shards(): lax.psum(shares[0].astype(jnp.bfloat16), 'rep').astype(jnp.float32)  154 us
    all_to_all x1, waiting for transfers between devices, shards(): lax.all_to_all(jnp.stack(jnp.split(outgoing, lax.axis_size('ep'), axis=0)...  96.1 us
    all_to_all x1, waiting for transfers between devices, shards(): lax.all_to_all(arrived_back[None], 'ep', split_axis=2, concat_axis=0, til...  93.1 us
    reduce_scatter x1, waiting for transfers between devices, shards(): lax.psum_scatter(query_weight_grad.astype(jnp.bfloat16), 'ep', scatter_di...  75.6 us
    reduce_scatter x1, waiting for transfers between devices, shards(): lax.psum_scatter(key_weight_grad.astype(jnp.bfloat16), 'ep', scatter_dime...  75 us
    reduce_scatter x1, waiting for transfers between devices, shards(): lax.psum_scatter(output_weight_grad.astype(jnp.bfloat16), 'ep', scatter_d...  74.9 us
    all_gather x1, waiting for transfers between devices, shards(): lax.all_gather(value_weight, 'ep', axis=0, tiled=True)  71 us
  transfers between devices with their start and end apart: 21, of which 15 were waited for; matrix products, arithmetic and copies ran while one was open for 20% of the time, Pallas kernels for 0%

profile of v1, /device:TPU:0, one launch (start us, length us, event | category | flops | bytes accessed | tf_op | source)
XLA Modules:
  0.0 1815.9 jit_solution(14201728191034140217)
XLA Ops:
  24.0 9.7 all-gather
  35.4 13.8 all-reduce.13
  49.2 9.2 all-gather.1
  69.8 8.1 all-to-all-done
  82.2 8.1 scatter_custom_fusion
  90.3 8.1 scatter_custom_fusion.2
  98.4 14.6 scatter_custom_fusion.1
  115.4 11.5 gather_fusion.2
  126.9 10.1 multiply_convert_fusion
  142.8 12.7 copy.114
  155.5 12.5 copy.115
  184.0 71.0 %all-gather.7.cloned.1.call-done = bf16[2048,2048]{1,0:T(8,128)(2,1)} async-done(((bf16[256,2048]{1,0:T(8,128)(2,1)}), bf16[2048,2048]{1,0:T(8,128)(2,1)}) %all-gather.7.cloned.1.call-update) | async-done | bytes 8388624 | tf_op jit(solution)/shard_map/all_gather | solution.py:97
  263.0 66.4 %all-gather.13.cloned.1.call-done = bf16[2048,2048]{1,0:T(8,128)(2,1)} async-done(((bf16[256,2048]{1,0:T(8,128)(2,1)}), bf16[2048,2048]{1,0:T(8,128)(2,1)}) %all-gather.13.cloned.1.call-update) | async-done | bytes 8388624 | tf_op jit(solution)/shard_map/all_gather | solution.py:98
  329.4 16.2 multiply_reduce_fusion.7
  347.1 9.9 gather_fusion
  357.0 8.0 broadcast_multiply_fusion
  383.0 9.2 copy.131
  392.2 96.1 %all-to-all-done.3 = bf16[8,1,2,144,2048]{4,3,2,1,0:T(8,128)(2,1)} async-done(((bf16[8,1,2,144,2048]{4,3,2,1,0:T(8,128)(2,1)}), bf16[8,1,2,144,2048]{4,3,2,1,0:T(8,128)(2,1)}, u32[]{:S(2)}, u32[]{:S(2)}) %all-to-all-start.3) | async-done | bytes 9437216 | tf_op jit(solution)/shard_map/all_to_all | solution.py:168
  488.3 9.3 copy.125
  497.5 27.3 %fusion.67 = f32[2,1152,2048]{2,1,0:T(8,128)} fusion(bf16[2,1152,2048]{2,1,0:T(8,128)(2,1)} %bitcast.192, bf16[2,2048,2048]{2,1,0:T(8,128)(2,1)} %param.28), kind=kOutput, calls=%fused_computation.174 | convolution fusion | flops 19327352832 | bytes 45088768 | tf_op jit(solution)/shard_map/erd,edf->erf/dot_general | solution.py:171
  524.9 27.5 %fusion.31 = (f32[2,1152,1024]{2,1,0:T(8,128)}, f32[2,1152,1024]{2,1,0:T(8,128)}, bf16[2,1152,1024]{2,1,0:T(8,128)(2,1)}) fusion(f32[2,1152,2048]{2,1,0:T(8,128)} %fusion.67, bf16[2,1152,2048]{2,1,0:T(8,128)(2,1)} %bitcast.194, bf16[2,1024,2048]{2,1,0:T(8,128)(2,1)} %param.29), kind=kOutput, calls=%fused_computation.95 | convolution fusion | flops 9696706560 | bytes 60293120 | tf_op jit(solution)/shard_map/erd,efd->erf/dot_general | solution.py:190
  552.4 14.6 fusion.4
  567.0 27.9 %copy.126 = bf16[1,2,1152,2048]{3,1,0,2:T(2,128)(2,1)} copy(bf16[1,2,1152,2048]{3,2,1,0:T(8,128)(2,1)S(1)} %fusion.4) | data formatting | bytes 18874368 | tf_op jit(solution)/shard_map/broadcast_in_dim | solution.py:182
  600.0 27.6 %fusion.5 = bf16[1,2,1152,2048]{3,2,1,0:T(8,128)(2,1)} fusion(bf16[2,2048,2048]{2,1,0:T(8,128)(2,1)} %param.28, f32[2,1152,1024]{2,1,0:T(8,128)} %get-tuple-element.37, f32[2,1152,1024]{2,1,0:T(8,128)} %get-tuple-element.36), kind=kOutput, calls=%fused_computation.22 | convolution fusion | flops 19341508608 | bytes 45088768 | tf_op jit(solution)/shard_map/erf,edf->erd/dot_general | solution.py:200
  627.6 18.2 %copy.132 = bf16[1,2,1152,2048]{3,1,0,2:T(2,128)(2,1)} copy(bf16[1,2,1152,2048]{3,2,1,0:T(8,128)(2,1)} %fusion.5) | data formatting | bytes 18874368 | tf_op jit(solution)/shard_map/broadcast_in_dim | solution.py:212
  645.9 59.4 %all-to-all-done.4 = bf16[1,2,1152,2048]{3,1,0,2:T(2,128)(2,1)} async-done(((bf16[1,2,1152,2048]{3,1,0,2:T(2,128)(2,1)}), bf16[1,2,1152,2048]{3,1,0,2:T(2,128)(2,1)}, u32[]{:S(2)}, u32[]{:S(2)}) %all-to-all-start.4) | async-done | bytes 9437216 | tf_op jit(solution)/shard_map/all_to_all | solution.py:181
  710.8 11.7 copy.127
  722.6 93.1 %all-to-all-done.8 = bf16[1,2,1152,2048]{3,1,0,2:T(2,128)(2,1)} async-done(((bf16[1,2,1152,2048]{3,1,0,2:T(2,128)(2,1)}), bf16[1,2,1152,2048]{3,1,0,2:T(2,128)(2,1)}, u32[]{:S(2)}, u32[]{:S(2)}) %all-to-all-start.8) | async-done | bytes 9437216 | tf_op jit(solution)/shard_map/all_to_all | solution.py:211
  815.6 11.8 copy.133
  827.4 21.2 %gather_fusion.1 = bf16[2048,2048]{1,0:T(8,128)(2,1)} fusion(bf16[2304,2048]{1,0:T(8,128)(2,1)} %bitcast.183, s32[2048]{0:T(1024)S(1)} %broadcast_clamp_fusion), kind=kCustom, calls=%fused_computation.1 | custom fusion | bytes 16785408 | tf_op jit(solution)/shard_map/gather | solution.py:184
  848.6 21.4 %gather_fusion.3 = bf16[2048,2048]{1,0:T(8,128)(2,1)} fusion(bf16[2304,2048]{1,0:T(8,128)(2,1)} %bitcast.184, s32[2048]{0:T(1024)S(1)} %broadcast_clamp_fusion), kind=kCustom, calls=%fused_computation.3 | custom fusion | bytes 16785408 | tf_op jit(solution)/shard_map/gather | solution.py:215
  870.0 11.4 convert_reduce_fusion
  883.6 12.9 fusion
  920.4 7.7 convolution_convert_fusion.3
  960.9 17.9 convolution_convert_fusion.7
  978.8 10.8 reduce-scatter.11.cloned.1.call-done
  989.6 74.9 %reduce-scatter.13.cloned.1.call-done = bf16[256,2048]{1,0:T(8,128)(2,1)} async-done(((bf16[2048,2048]{1,0:T(8,128)(2,1)}), bf16[256,2048]{1,0:T(8,128)(2,1)}) %reduce-scatter.13.cloned.1.call-update) | async-done | bytes 1048592 | tf_op jit(solution)/shard_map/reduce_scatter | solution.py:280
  1064.5 75.0 %reduce-scatter.9.cloned.1.call-done = bf16[256,2048]{1,0:T(8,128)(2,1)} async-done(((bf16[2048,2048]{1,0:T(8,128)(2,1)}), bf16[256,2048]{1,0:T(8,128)(2,1)}) %reduce-scatter.9.cloned.1.call-update) | async-done | bytes 1048592 | tf_op jit(solution)/shard_map/reduce_scatter | solution.py:274
  1139.5 75.6 %reduce-scatter.7.cloned.1.call-done = bf16[256,2048]{1,0:T(8,128)(2,1)} async-done(((bf16[2048,2048]{1,0:T(8,128)(2,1)}), bf16[256,2048]{1,0:T(8,128)(2,1)}) %reduce-scatter.7.cloned.1.call-update) | async-done | bytes 1048592 | tf_op jit(solution)/shard_map/reduce_scatter | solution.py:271
  1215.2 29.3 %convolution_convert_fusion = bf16[2,2048,2048]{2,1,0:T(8,128)(2,1)} fusion(bf16[2,1152,2048]{2,1,0:T(8,128)(2,1)} %bitcast.193, f32[2,1152,1024]{2,1,0:T(8,128)} %get-tuple-element.37, f32[2,1152,1024]{2,1,0:T(8,128)} %get-tuple-element.36), kind=kOutput, calls=%fused_computation.13 | convolution fusion | flops 19345178624 | bytes 45088768 | tf_op jit(solution)/shard_map/erd,erf->edf/dot_general | solution.py:197
  1263.4 8.0 reduce.8
  1279.9 6.8 reduce.7
  1298.5 21.1 %all-reduce.12 = (bf16[2048]{0:T(1024)(128)(2,1)S(1)}, bf16[2048]{0:T(1024)(128)(2,1)S(1)}, bf16[128]{0:T(256)(128)(2,1)S(1)}, bf16[128]{0:T(256)(128)(2,1)S(1)}) all-reduce(bf16[2048]{0:T(1024)(128)(2,1)S(1)} %get-tuple-element.18, bf16[2048]{0:T(1024)(128)(2,1)S(1)} %get-tuple-element.16, ...), channel_id=6, replica_groups=mesh['rep'=4,'ep'=8] {'ep'}, use_global_device_ids=true, to_apply=%region_28.29.clone | all-reduce | flops 4352 | bytes 17408
  1320.0 12.4 all-reduce.14
  1343.1 19.3 %reduce-scatter.17.cloned.1.call-done = bf16[2,256,2048]{2,1,0:T(8,128)(2,1)} async-done(((bf16[2,1024,2048]{2,1,0:T(8,128)(2,1)}), bf16[2,256,2048]{2,1,0:T(8,128)(2,1)}) %reduce-scatter.17.cloned.1.call-update) | async-done | bytes 2097168 | tf_op jit(solution)/shard_map/reduce_scatter | solution.py:207
  1366.5 153.9 %all-reduce.18.cloned.1.call-done = (bf16[256,2048]{1,0:T(8,128)(2,1)}, bf16[256,2048]{1,0:T(8,128)(2,1)}, bf16[256,2048]{1,0:T(8,128)(2,1)}, bf16[256,2048]{1,0:T(8,128)(2,1)}) async-done(((bf16[256,2048]{1,0:T(8,128)(2,1)}, bf16[256,2048]{1,0:T(8,128)(2,1)}, bf16[256,2048]{1,0:T(8,128)(2,1)}, bf16[256,2048]{1,0:T(8,128)(2,1)}), (bf16[256,2048]{1,0:T(8,128)(2,1)}, bf16[256,2048]{1,0:T(8,128)(2,1)}, ...) | async-done | bytes 4194320 | tf_op jit(solution)/shard_map/psum | solution.py:297
  1529.3 273.0 %reduce-scatter.15.cloned.1.call-done = bf16[2,512,2048]{2,1,0:T(8,128)(2,1)} async-done(((bf16[2,2048,2048]{2,1,0:T(8,128)(2,1)}), bf16[2,512,2048]{2,1,0:T(8,128)(2,1)}) %reduce-scatter.15.cloned.1.call-update) | async-done | bytes 4194320 | tf_op jit(solution)/shard_map/reduce_scatter | solution.py:204
  1802.3 6.7 convert_element_type.294
  (330 shorter events, 214.9 us)
Async XLA Ops:
  7.2 26.5 %copy-start.73 = (u32[32]{0:T(128)S(1)}, u32[32]{0:T(128)}, u32[]{:S(2)}) copy-start(u32[32]{0:T(128)} %constant.91) | copy-start | bytes 388
  7.2 16.7 copy-start.74
  7.2 27.7 %copy-start.75 = (bf16[16]{0:T(256)(128)(2,1)S(1)}, bf16[16]{0:T(256)(128)(2,1)}, u32[]{:S(2)}) copy-start(bf16[16]{0:T(256)(128)(2,1)} %param.26) | copy-start | bytes 100
  7.2 28.0 %copy-start.76 = (bf16[16]{0:T(256)(128)(2,1)S(1)}, bf16[16]{0:T(256)(128)(2,1)}, u32[]{:S(2)}) copy-start(bf16[16]{0:T(256)(128)(2,1)} %param.27) | copy-start | bytes 100
  7.2 42.0 %copy-start.77 = (bf16[256]{0:T(256)(128)(2,1)S(1)}, bf16[256]{0:T(256)(128)(2,1)}, u32[]{:S(2)}) copy-start(bf16[256]{0:T(256)(128)(2,1)} %param.25) | copy-start | bytes 1540
  7.3 135.5 %all-gather.9.cloned.1.call-start = ((), (), s32[]{:S(2)}) async-start(), calls=%async_computation.17 | async-start | bytes 9437184 | tf_op jit(solution)/shard_map/all_gather | solution.py:95
  8.0 147.5 %all-gather.11.cloned.1.call-start = ((), (), s32[]{:S(2)}) async-start(), calls=%async_computation.18 | async-start | bytes 9437184 | tf_op jit(solution)/shard_map/all_gather | solution.py:96
  8.7 246.2 %all-gather.7.cloned.1.call-start = ((), (), s32[]{:S(2)}) async-start(), calls=%async_computation.16 | async-start | bytes 9437184 | tf_op jit(solution)/shard_map/all_gather | solution.py:97
  9.5 319.9 %all-gather.13.cloned.1.call-start = ((), (), s32[]{:S(2)}) async-start(), calls=%async_computation.19 | async-start | bytes 9437184 | tf_op jit(solution)/shard_map/all_gather | solution.py:98
  10.7 9.8 all-to-all-start.1
  17.9 311.5 %copy-start.59 = (f32[256]{0:T(256)}, f32[256]{0:T(256)S(1)}, u32[]{:S(2)}) copy-start(f32[256]{0:T(256)S(1)} %compare_convert_fusion) | copy-start | bytes 3076
  20.6 38.4 %all-to-all-start.2 = ((s32[8,1,256]{2,1,0:T(1,128)}), s32[8,1,256]{2,1,0:T(1,128)S(1)}, u32[]{:S(2)}, u32[]{:S(2)}) async-start(s32[8,1,256]{2,1,0:T(1,128)} %reshape.522), calls=%async_computation.2 | async-start | bytes 16384 | tf_op jit(solution)/shard_map/all_to_all | solution.py:85
  23.9 236.9 %copy-start.67 = (pred[256]{0:T(512)(128)(4,1)}, pred[256]{0:T(512)(128)(4,1)S(1)}, u32[]{:S(2)}) copy-start(pred[256]{0:T(512)(128)(4,1)S(1)} %broadcast_compare_fusion) | copy-start | bytes 772
  33.6 108.8 %copy-start.45 = (f32[8,1,256]{2,1,0:T(1,128)}, f32[8,1,256]{2,1,0:T(1,128)S(1)}, u32[]{:S(2)}) copy-start(f32[8,1,256]{2,1,0:T(1,128)S(1)} %convert_element_type.303) | copy-start | bytes 24580
  49.2 128.4 %copy-start.69 = (f32[128]{0:T(128)}, f32[128]{0:T(128)S(1)}, u32[]{:S(2)}) copy-start(f32[128]{0:T(128)S(1)} %convert_element_type.242) | copy-start | bytes 1540
  49.2 128.3 %copy-start.71 = (f32[128]{0:T(128)}, f32[128]{0:T(128)S(1)}, u32[]{:S(2)}) copy-start(f32[128]{0:T(128)S(1)} %convert_element_type.244) | copy-start | bytes 1540
  58.5 287.1 %copy-start.47 = (f32[8,1,256]{2,1,0:T(1,128)}, f32[8,1,256]{2,1,0:T(1,128)S(1)}, u32[]{:S(2)}) copy-start(f32[8,1,256]{2,1,0:T(1,128)S(1)} %convert_element_type.304) | copy-start | bytes 24580
  59.0 18.9 %all-to-all-start = ((bf16[8,32,2048]{2,1,0:T(8,128)(2,1)}), bf16[8,32,2048]{2,1,0:T(8,128)(2,1)S(1)}, u32[]{:S(2)}, u32[]{:S(2)}) async-start(bf16[8,32,2048]{2,1,0:T(8,128)(2,1)} %param.15), calls=%async_computation | async-start | bytes 2097152 | tf_op jit(solution)/shard_map/all_to_all | solution.py:78
  77.9 251.5 %copy-start.3 = (bf16[8,32,2048]{2,1,0:T(8,128)(2,1)}, bf16[8,32,2048]{2,1,0:T(8,128)(2,1)S(1)}, u32[]{:S(2)}) copy-start(bf16[8,32,2048]{2,1,0:T(8,128)(2,1)S(1)} %all-to-all-done) | copy-start | bytes 3145732
  77.9 36.1 %all-to-all-start.6 = ((bf16[8,32,2048]{2,1,0:T(8,128)(2,1)}), bf16[8,32,2048]{2,1,0:T(8,128)(2,1)}, u32[]{:S(2)}, u32[]{:S(2)}) async-start(bf16[8,32,2048]{2,1,0:T(8,128)(2,1)} %param.16), calls=%async_computation.6 | async-start | bytes 2097152 | tf_op jit(solution)/shard_map/all_to_all | solution.py:79
  82.2 16.3 copy-start.54
  114.0 28.1 %copy-start.61 = (f32[256]{0:T(256)}, f32[256]{0:T(256)S(1)}, u32[]{:S(2)}) copy-start(f32[256]{0:T(256)S(1)} %rsqrt.45) | copy-start | bytes 3076
  137.0 241.0 %all-to-all-start.7 = ((bf16[8,2,144,2048]{3,2,1,0:T(8,128)(2,1)}), bf16[8,2,144,2048]{3,2,1,0:T(8,128)(2,1)}, u32[]{:S(2)}, u32[]{:S(2)}) async-start(bf16[8,2,144,2048]{3,2,1,0:T(8,128)(2,1)} %multiply_convert_fusion), calls=%async_computation.7 | async-start | bytes 18874368 | tf_op jit(solution)/shard_map/all_to_all | solution.py:189
  142.7 31.8 %copy-start.7 = (bf16[8,32,2048]{2,1,0:T(8,128)(2,1)}, bf16[8,32,2048]{2,1,0:T(8,128)(2,1)S(1)}, u32[]{:S(2)}) copy-start(bf16[8,32,2048]{2,1,0:T(8,128)(2,1)S(1)} %fusion.28) | copy-start | bytes 3145732
  183.9 76.9 %copy-start.41 = (f32[16,256]{1,0:T(8,128)}, f32[16,256]{1,0:T(8,128)S(1)}, u32[]{:S(2)}) copy-start(f32[16,256]{1,0:T(8,128)S(1)} %log_add_fusion) | copy-start | bytes 49156
  263.0 82.6 %copy-start.21 = (bf16[16,128,256]{2,1,0:T(8,128)(2,1)}, bf16[16,128,256]{2,1,0:T(8,128)(2,1)S(1)}, u32[]{:S(2)}) copy-start(bf16[16,128,256]{2,1,0:T(8,128)(2,1)S(1)} %convolution_convert_fusion.11) | copy-start | bytes 3145732
  345.6 11.4 copy-start.63
  345.6 11.4 copy-start.56
  378.0 110.3 %all-to-all-start.3 = ((bf16[8,1,2,144,2048]{4,3,2,1,0:T(8,128)(2,1)}), bf16[8,1,2,144,2048]{4,3,2,1,0:T(8,128)(2,1)}, u32[]{:S(2)}, u32[]{:S(2)}) async-start(bf16[8,1,2,144,2048]{4,3,2,1,0:T(8,128)(2,1)} %constant_dynamic-update-slice_fusion), calls=%async_computation.3 | async-start | bytes 18874368 | tf_op jit(solution)/shard_map/all_to_all | solution.py:168
  594.9 110.4 %all-to-all-start.4 = ((bf16[1,2,1152,2048]{3,1,0,2:T(2,128)(2,1)}), bf16[1,2,1152,2048]{3,1,0,2:T(2,128)(2,1)}, u32[]{:S(2)}, u32[]{:S(2)}) async-start(bf16[1,2,1152,2048]{3,1,0,2:T(2,128)(2,1)} %copy.126), calls=%async_computation.4 | async-start | bytes 18874368 | tf_op jit(solution)/shard_map/all_to_all | solution.py:181
  645.9 64.7 %copy-start.44 = (bf16[8,8,32]{2,1,0:T(8,128)(2,1)S(1)}, bf16[8,8,32]{2,1,0:T(8,128)(2,1)}, u32[]{:S(2)}) copy-start(bf16[8,8,32]{2,1,0:T(8,128)(2,1)} %copy-done.43) | copy-start | bytes 12292
  645.9 64.8 %copy-start.60 = (f32[256]{0:T(256)S(1)}, f32[256]{0:T(256)}, u32[]{:S(2)}) copy-start(f32[256]{0:T(256)} %copy-done.59) | copy-start | bytes 3076
  645.9 64.9 %copy-start.55 = (s32[2048,1]{0,1:T(1,128)S(1)}, s32[2048,1]{0,1:T(1,128)}, u32[]{:S(2)}) copy-start(s32[2048,1]{0,1:T(1,128)} %copy-done.54) | copy-start | bytes 24580
  705.3 110.3 %all-to-all-start.8 = ((bf16[1,2,1152,2048]{3,1,0,2:T(2,128)(2,1)}), bf16[1,2,1152,2048]{3,1,0,2:T(2,128)(2,1)}, u32[]{:S(2)}, u32[]{:S(2)}) async-start(bf16[1,2,1152,2048]{3,1,0,2:T(2,128)(2,1)} %copy.132), calls=%async_computation.8 | async-start | bytes 18874368 | tf_op jit(solution)/shard_map/all_to_all | solution.py:211
  710.3 279.3 %reduce-scatter.11.cloned.1.call-start = ((), (), s32[]{:S(2)}) async-start(), calls=%async_computation.22 | async-start | bytes 9437184 | tf_op jit(solution)/shard_map/reduce_scatter | solution.py:277
  870.0 11.5 copy-start.6
  870.0 11.4 copy-start.48
  870.0 11.4 copy-start.57
  918.8 145.7 %reduce-scatter.13.cloned.1.call-start = ((), (), s32[]{:S(2)}) async-start(), calls=%async_computation.23 | async-start | bytes 9437184 | tf_op jit(solution)/shard_map/reduce_scatter | solution.py:280
  928.1 211.4 %reduce-scatter.9.cloned.1.call-start = ((), (), s32[]{:S(2)}) async-start(), calls=%async_computation.21 | async-start | bytes 9437184 | tf_op jit(solution)/shard_map/reduce_scatter | solution.py:274
  951.1 264.0 %reduce-scatter.7.cloned.1.call-start = ((), (), s32[]{:S(2)}) async-start(), calls=%async_computation.20 | async-start | bytes 9437184 | tf_op jit(solution)/shard_map/reduce_scatter | solution.py:271
  960.8 401.6 %reduce-scatter.17.cloned.1.call-start = ((), (), s32[]{:S(2)}) async-start(), calls=%async_computation.25 | async-start | bytes 10485760 | tf_op jit(solution)/shard_map/reduce_scatter | solution.py:207
  978.8 541.6 %all-reduce.18.cloned.1.call-start = ((), (), s32[]{:S(2)}) async-start(), calls=%async_computation.26 | async-start | bytes 8388608 | tf_op jit(solution)/shard_map/psum | solution.py:297
  1215.1 587.1 %reduce-scatter.15.cloned.1.call-start = ((), (), s32[]{:S(2)}) async-start(), calls=%async_computation.24 | async-start | bytes 20971520 | tf_op jit(solution)/shard_map/reduce_scatter | solution.py:204
  1245.8 12.0 slice-start
  1262.9 15.4 copy-start.22
  1274.0 19.6 %all-to-all-start.9 = ((bf16[8,2,32768]{2,1,0:T(2,128)(2,1)}), bf16[8,2,32768]{2,1,0:T(2,128)(2,1)}, u32[]{:S(2)}, u32[]{:S(2)}) async-start(bf16[8,2,32768]{2,1,0:T(2,128)(2,1)} %reshape.528), calls=%async_computation.9 | async-start | bytes 2097152 | tf_op jit(solution)/shard_map/all_to_all | solution.py:268
  1293.7 46.8 %all-to-all-start.5 = ((bf16[8,2,32768]{2,1,0:T(2,128)(2,1)}), bf16[8,2,32768]{2,1,0:T(2,128)(2,1)S(1)}, u32[]{:S(2)}, u32[]{:S(2)}) async-start(bf16[8,2,32768]{2,1,0:T(2,128)(2,1)} %reshape.526), calls=%async_computation.5 | async-start | bytes 2097152 | tf_op jit(solution)/shard_map/all_to_all | solution.py:265
  (53 other events, 179.0 us)
Sparse Core Ops, SparseCore 0:
  9.9 57.3 all-gather.8
  69.2 65.4 all-gather.10
  136.5 118.3 all-gather.6
  256.7 72.6 all-gather.12
  919.0 70.6 reduce-scatter.10
  993.0 71.5 reduce-scatter.12
  1068.0 71.5 reduce-scatter.8
  1143.6 71.5 reduce-scatter.6
  1217.5 144.8 reduce-scatter.16
  1364.8 155.5 all-reduce.17
  1522.8 279.4 reduce-scatter.14
